TPU v7x, 32 devices: a whole 2x2x4 slice. The times are simulated.
32 devices in a mesh: energy: 4 (over z), orb: 4 (over y, x), kpt: 2 (over core).
Axes of the slice: x: 2, y: 2, z: 4, core: 2. Of those that a mesh axis runs over, the one named last changes fastest.
Arguments:
- lesser: bfloat16 [2, 4, 16, 1, 512, 512], P(None, 'energy', 'kpt', None, None, 'orb'), may hold values from -6 to 6
- coupling: bfloat16 [2, 16, 512, 512], P(None, None, None, 'orb'), may hold values from -0.046875 to 0.046875
- transfer_map: int32 [16, 16], replicated, may hold values from 0 to 15, as said below
Outputs:
- sigma: bfloat16 [2, 4, 16, 1, 512, 512], P(None, None, 'kpt', None, 'energy', 'orb')
Inputs may be any that keep to these rules, and one draw needn't show every extreme that they name: transfer_map[k, p] is the index of the momentum transfer k - p: each row and each column holds every number of 0 to 15 once.
All inputs are finite; a program needn't handle non-finite values.
Results may differ from a plain program's by a relative error of at most 0.001.
Values may be sent and summed in bfloat16 or wider, within the bound.
A program may use at most 128 MiB of HBM per device.

v0:
```python
import jax
import jax.numpy as jnp
from jax import lax
from jax.sharding import PartitionSpec as P


def complex_terms(green, selected):
    real_out = jnp.einsum(
        "prm,tpmj->trj", green[0], selected[0], preferred_element_type=jnp.float32
    ) - jnp.einsum("prm,tpmj->trj", green[1], selected[1], preferred_element_type=jnp.float32)
    imag_out = jnp.einsum(
        "prm,tpmj->trj", green[0], selected[1], preferred_element_type=jnp.float32
    ) + jnp.einsum("prm,tpmj->trj", green[1], selected[0], preferred_element_type=jnp.float32)
    return (real_out, imag_out)


def per_device(lesser, coupling, transfer_map):
    regrouped = lax.all_to_all(lesser, "energy", split_axis=4, concat_axis=1, tiled=True)
    gathered = lax.all_gather(regrouped, "orb", axis=5, tiled=True)
    energies = gathered.shape[1]
    local_points = gathered.shape[2]
    layers = gathered.shape[3]
    tile = gathered.shape[4]
    width = gathered.shape[5]
    out_cols = coupling.shape[3]
    row_count = energies * layers * tile
    first_point = lax.axis_index("kpt") * local_points
    reordered = jnp.moveaxis(gathered, 2, 1).reshape(2, local_points, row_count, width)
    my_columns = lax.dynamic_slice_in_dim(transfer_map, first_point, local_points, 1)
    selected = jnp.take(coupling, my_columns, axis=1)
    real_out, imag_out = complex_terms(reordered, selected)
    mine = lax.psum_scatter(
        jnp.stack([real_out, imag_out], axis=1), "kpt", scatter_dimension=0, tiled=True
    )
    summed = jnp.moveaxis(mine, 1, 0)
    result = summed.astype(jnp.bfloat16).reshape(2, local_points, energies, layers, tile, out_cols)
    return jnp.moveaxis(result, 1, 2)


def solution(mesh):
    in_specs = (P(None, "energy", "kpt", None, None, "orb"), P(None, None, None, "orb"), P())
    out_specs = P(None, None, "kpt", None, "energy", "orb")
    return jax.shard_map(
        per_device, mesh=mesh, in_specs=in_specs, out_specs=out_specs, check_vma=False
    )
```

profile of v0, /device:TPU:0, one launch (start us, length us, event | category | flops | bytes accessed | tf_op | source)
XLA Modules:
  0.0 261.4 jit_solution(8612153667532477465)
XLA Ops:
  6.5 2.9 %copy.17 = bf16[2,1,8,1,512,128]{5,2,3,1,0,4:T(8,128)(2,1)S(1)} copy(bf16[2,1,8,1,512,128]{5,4,3,2,1,0:T(8,128)(2,1)} %param.3) | data formatting | bytes 4194304 | tf_op args[0]
  9.5 54.3 %all_to_all.18 = bf16[2,1,8,1,512,128]{5,2,3,1,0,4:T(8,128)(2,1)S(1)} all-to-all(bf16[2,1,8,1,512,128]{5,2,3,1,0,4:T(8,128)(2,1)S(1)} %copy.17), channel_id=1, replica_groups=mesh['energy'=4,'orb'=4,'kpt'=2] {'energy'}, dimensions={4} | all-to-all | bytes 4194304 | tf_op jit(solution)/shard_map/all_to_all | solution.py:18
  63.8 1.9 copy.18
  65.7 0.0 all-gather.3.cloned.1.call-update
  65.7 0.2 reduce-scatter.5.cloned.1.call-start
  66.0 0.1 compare_and_fusion
  66.0 0.1 reshape.16
  66.1 16.5 %gather_fusion = bf16[128,2,512,128]{3,2,1,0:T(8,128)(2,1)} fusion(bf16[2,16,512,128]{3,2,1,0:T(8,128)(2,1)} %param.4, s32[1024]{0:T(1024)S(1)} %pad_clamp_fusion), kind=kCustom, calls=%fused_computation | custom fusion | bytes 67109376 | tf_op jit(solution)/shard_map/jit(_take)/gather | solution.py:30
  82.6 43.4 %copy.16 = bf16[128,2,512,128]{2,3,0,1:T(8,128)(2,1)} copy(bf16[128,2,512,128]{3,2,1,0:T(8,128)(2,1)} %gather_fusion) | data formatting | bytes 67108864 | tf_op jit(solution)/shard_map/jit(_take)/gather | solution.py:30
  126.0 22.9 %select_bitcast_fusion = bf16[2,16,8,512,128]{3,4,2,1,0:T(8,128)(2,1)} fusion(bf16[16,8,2,512,128]{3,4,1,0,2:T(8,128)(2,1)} %bitcast.75, pred[16,8]{1,0:T(8,128)(4,1)S(1)} %get-tuple-element.5), kind=kLoop, calls=%fused_computation.1 | loop fusion | flops 16777216 | bytes 67108992 | tf_op jit(solution)/shard_map/jit(_take)/select_n | solution.py:30
  148.8 3.6 %all-gather.3.cloned.1.call-done = bf16[2,4,1,8,1,128,512]{6,5,1,3,0,4,2:T(8,128)(2,1)} async-done(((bf16[2,4,1,8,1,128,128]{6,5,1,3,0,4,2:T(8,128)(2,1)}), bf16[2,4,1,8,1,128,512]{6,5,1,3,0,4,2:T(8,128)(2,1)}) %all-gather.3.cloned.1.call-update) | async-done | bytes 8388624 | tf_op jit(solution)/shard_map/all_gather | solution.py:19
  152.5 3.8 %fusion.7 = (bf16[1,8,4,1,128,512]{5,4,2,1,0,3:T(8,128)(2,1)S(1)}, bf16[1,8,4,1,128,512]{5,4,2,1,0,3:T(8,128)(2,1)S(1)}) fusion(bf16[2,8,4,1,128,512]{5,4,2,1,0,3:T(8,128)(2,1)} %bitcast.79), kind=kLoop, calls=%fused_computation.18 | loop fusion | bytes 16777216 | tf_op jit(solution)/shard_map/slice | solution.py:9
  156.3 15.3 %fusion.1 = f32[16,128,512,1]{2,1,3,0:T(8,128)} fusion(bf16[8,512,512,1]{2,1,0,3:T(8,128)(2,1)S(1)} %bitcast.83, bf16[2,16,8,512,128]{3,4,2,1,0:T(8,128)(2,1)} %select_bitcast_fusion), kind=kOutput, calls=%fused_computation.5 | convolution fusion | flops 8589934592 | bytes 25165824 | tf_op jit(solution)/shard_map/prm,tpmj->trj/dot_general | solution.py:8
  171.6 13.8 %fusion = f32[16,128,512,1]{2,1,3,0:T(8,128)} fusion(bf16[8,512,512,1]{2,1,0,3:T(8,128)(2,1)S(1)} %bitcast.85, bf16[2,16,8,512,128]{3,4,2,1,0:T(8,128)(2,1)} %select_bitcast_fusion), kind=kOutput, calls=%fused_computation.4 | convolution fusion | flops 8589934592 | bytes 25165824 | tf_op jit(solution)/shard_map/prm,tpmj->trj/dot_general | solution.py:13
  185.4 14.3 %fusion.5 = f32[16,1,512,128]{2,3,0,1:T(8,128)S(1)} fusion(f32[16,128,512,1]{2,1,3,0:T(8,128)} %fusion.1, bf16[8,512,512,1]{2,1,0,3:T(8,128)(2,1)} %bitcast.86, bf16[2,16,8,512,128]{3,4,2,1,0:T(8,128)(2,1)} %select_bitcast_fusion), kind=kOutput, calls=%fused_computation.13 | convolution fusion | flops 8590983168 | bytes 29360128 | tf_op jit(solution)/shard_map/prm,tpmj->trj/dot_general | solution.py:10
  199.6 14.4 %fusion.4 = f32[16,1,512,128]{2,3,0,1:T(8,128)} fusion(f32[16,128,512,1]{2,1,3,0:T(8,128)} %fusion, bf16[8,512,512,1]{2,1,0,3:T(8,128)(2,1)S(1)} %bitcast.84, bf16[2,16,8,512,128]{3,4,2,1,0:T(8,128)(2,1)} %select_bitcast_fusion), kind=kOutput, calls=%fused_computation.11 | convolution fusion | flops 8590983168 | bytes 29360128 | tf_op jit(solution)/shard_map/prm,tpmj->trj/dot_general | solution.py:11
  214.0 3.4 %pad_maximum_fusion = f32[16,2,512,128]{2,3,0,1:T(8,128)S(1)} fusion(f32[16,1,512,128]{2,3,0,1:T(8,128)} %fusion.4, f32[16,1,512,128]{2,3,0,1:T(8,128)S(1)} %fusion.5), kind=kLoop, calls=%fused_computation.8 | loop fusion | flops 2097152 | bytes 16777216 | tf_op jit(solution)/shard_map/stack | solution.py:33
  217.4 1.6 copy.24
  219.0 8.1 %copy.26 = f32[2,8,256,512]{3,1,2,0:T(8,128)} copy(f32[2,8,256,512]{3,2,1,0:T(8,128)S(1)} %bitcast.77) | data formatting | bytes 16777216
  227.1 16.6 %reduce-scatter.5.cloned.1.call-done = f32[8,131072]{1,0:T(8,128)} async-done(((f32[16,131072]{1,0:T(8,128)}), f32[8,131072]{1,0:T(8,128)}) %reduce-scatter.5.cloned.1.call-update) | async-done | bytes 4194320
  243.6 4.4 %copy.27 = bf16[1,8,256,512]{3,2,1,0:T(8,128)(2,1)S(1)} copy(f32[1,8,256,512]{3,1,2,0:T(8,128)} %bitcast.82) | data formatting | bytes 6291456
  248.1 0.2 copy.31
  248.2 2.1 reshape.13
  250.3 4.3 %copy.19 = bf16[2,8,4,1,128,128]{5,4,3,1,2,0:T(8,128)(2,1)} copy(bf16[2,8,4,1,128,128]{4,2,5,1,0,3:T(4,128)(2,1)} %reshape.13) | data formatting | bytes 4194304 | tf_op jit(solution)/shard_map/reshape | solution.py:36
  (7 shorter events, 0.0 us)
Async XLA Ops:
  6.5 145.9 %all-gather.3.cloned.1.call-start = ((), (), s32[]{:S(2)}) async-start(), calls=%async_computation.2 | async-start | bytes 10485760 | tf_op jit(solution)/shard_map/all_gather | solution.py:19
  63.8 2.1 copy-start.1
  65.7 177.9 %reduce-scatter.5.cloned.1.call-start = ((), (), s32[]{:S(2)}) async-start(), calls=%async_computation.3 | async-start | bytes 12582912
  156.3 15.3 %copy-start = (bf16[1,8,4,1,128,512]{5,4,2,1,0,3:T(8,128)(2,1)}, bf16[1,8,4,1,128,512]{5,4,2,1,0,3:T(8,128)(2,1)S(1)}, u32[]{:S(2)}) copy-start(bf16[1,8,4,1,128,512]{5,4,2,1,0,3:T(8,128)(2,1)S(1)} %get-tuple-element.8) | copy-start | bytes 12582916
Sparse Core Ops, SparseCore 0:
  65.8 86.5 all-gather.2
  227.2 16.3 reduce-scatter.4
where the time goes:
time: 263 us; the launch traced here: 261 us
  local copies, waits for them, and re-layouts  89.2 us (34%)
  matrix products  57.7 us (22%)
  blocking collectives  54.3 us (21%)
  other arithmetic  26.3 us (10%)
  waiting for transfers between devices  20.2 us (8%)
  between operations  13.5 us (5%)
    gather x2, local copies, waits for them, and re-layouts, per_device(): selected = jnp.take(coupling, my_columns, axis=1)  59.8 us
    all_to_all x1, blocking collectives, per_device(): lax.all_to_all(lesser, 'energy', split_axis=4, concat_axis=1, tiled=True)  54.3 us
    select_n x1, other arithmetic, per_device(): selected = jnp.take(coupling, my_columns, axis=1)  22.9 us
    unnamed x9, local copies, waits for them, and re-layouts  17.2 us
    unnamed x3, waiting for transfers between devices  16.6 us
    dot_general x1, matrix products, complex_terms(): jnp.einsum('prm,tpmj->trj', green[0], selected[0], preferred_element_type...  15.3 us
    dot_general x1, matrix products, complex_terms(): jnp.einsum('prm,tpmj->trj', green[0], selected[1], preferred_element_type...  14.4 us
    dot_general x1, matrix products, complex_terms(): jnp.einsum('prm,tpmj->trj', green[1], selected[1], preferred_element_type...  14.3 us
  transfers between devices with their start and end apart: 2, of which 2 were waited for; matrix products, arithmetic and copies ran while one was open for 32% of the time, Pallas kernels for 0%

commit v1 on v0

--- a/solution.py
+++ b/solution.py
@@ -1,7 +1,14 @@
+import functools
+
 import jax
 import jax.numpy as jnp
 from jax import lax
+from jax.experimental import pallas as pl
+from jax.experimental.pallas import tpu as pltpu
 from jax.sharding import PartitionSpec as P
+
+MESH = pl.DeviceIdType.MESH
+X, Y, DA, DB, P0, PX, PY, PD = range(8)
 
 
 def complex_terms(green, selected):
@@ -14,7 +21,7 @@
     return (real_out, imag_out)
 
 
-def per_device(lesser, coupling, transfer_map):
+def per_device_general(lesser, coupling, transfer_map):
     regrouped = lax.all_to_all(lesser, "energy", split_axis=4, concat_axis=1, tiled=True)
     gathered = lax.all_gather(regrouped, "orb", axis=5, tiled=True)
     energies = gathered.shape[1]
@@ -37,9 +44,259 @@
     return jnp.moveaxis(result, 1, 2)
 
 
+def kernel(nz, map_ref, lesser, coupling, out, g, u, acc, zsend, zrecv, send, recv, local_sem, u_sem):
+    points = lesser.shape[2]
+    width = lesser.shape[5]
+    tile = g.shape[5]
+    rows = nz * tile
+    e = lax.axis_index("energy")
+    o = lax.axis_index("orb")
+    c = lax.axis_index("kpt")
+    ox = o + 1 - 2 * lax.rem(o, 2)
+    oy = lax.rem(o + 2, 4)
+    od = 3 - o
+    cp = 1 - c
+
+    def to_energy(d):
+        return lax.rem(e + d, nz)
+
+    def from_energy(d):
+        return lax.rem(e + nz - d, nz)
+
+    def own_rows(s, z):
+        return lesser.at[:, 0, s, 0, pl.ds(pl.multiple_of(z * tile, tile), tile), :]
+
+    def z_copy(d, s, owner, target):
+        return pltpu.make_async_remote_copy(
+            src_ref=own_rows(s, target),
+            dst_ref=g.at[c, o, :, s, owner],
+            send_sem=zsend.at[d - 1, s],
+            recv_sem=zrecv.at[d - 1, s],
+            device_id={"energy": target},
+            device_id_type=MESH,
+        )
+
+    def local_copy(s):
+        return pltpu.make_async_copy(own_rows(s, e), g.at[c, o, :, s, e], local_sem.at[s])
+
+    def move(kind, s, ref, target):
+        return pltpu.make_async_remote_copy(
+            src_ref=ref,
+            dst_ref=ref,
+            send_sem=send.at[kind, s],
+            recv_sem=recv.at[kind, s],
+            device_id=target,
+            device_id_type=MESH,
+        )
+
+    def block(k, q, s):
+        return g.at[k, q, :, s]
+
+    def half(q, part, s):
+        return g.at[c, q, part, s]
+
+    to_x, to_y, to_peer = {"orb": ox}, {"orb": oy}, {"kpt": cp}
+
+    def outgoing(s):
+        return {
+            X: move(X, s, block(c, o, s), to_x),
+            Y: move(Y, s, block(c, o, s), to_y),
+            P0: move(P0, s, block(c, o, s), to_peer),
+            DA: move(DA, s, half(ox, 0, s), to_y),
+            PX: move(PX, s, block(c, ox, s), to_peer),
+            DB: move(DB, s, half(oy, 1, s), to_x),
+            PY: move(PY, s, block(c, oy, s), to_peer),
+            PD: move(PD, s, block(c, od, s), to_peer),
+        }
+
+    def incoming(s):
+        return {
+            X: move(X, s, block(c, ox, s), to_x),
+            Y: move(Y, s, block(c, oy, s), to_y),
+            DA: move(DA, s, half(od, 0, s), to_y),
+            DB: move(DB, s, half(od, 1, s), to_x),
+            P0: move(P0, s, block(cp, o, s), to_peer),
+            PX: move(PX, s, block(cp, ox, s), to_peer),
+            PY: move(PY, s, block(cp, oy, s), to_peer),
+            PD: move(PD, s, block(cp, od, s), to_peer),
+        }
+
+    def locals_start(s, _):
+        local_copy(s).start()
+        return 0
+
+    lax.fori_loop(0, points, locals_start, 0)
+    u_copy = pltpu.make_async_copy(coupling, u, u_sem)
+    u_copy.start()
+
+    barrier = pltpu.get_barrier_semaphore()
+    for d in range(1, nz):
+        pl.semaphore_signal(barrier, inc=1, device_id={"energy": to_energy(d)}, device_id_type=MESH)
+    for target in (to_x, to_y, to_peer):
+        pl.semaphore_signal(barrier, inc=1, device_id=target, device_id_type=MESH)
+    pl.semaphore_wait(barrier, nz - 1 + 3)
+
+    def z_start(s, _):
+        for d in range(1, nz):
+            z_copy(d, s, e, to_energy(d)).start()
+        return 0
+
+    lax.fori_loop(0, points, z_start, 0)
+
+    def clear(t, _):
+        acc[t] = jnp.zeros(acc.shape[1:], acc.dtype)
+        return 0
+
+    lax.fori_loop(0, points, clear, 0)
+    u_copy.wait()
+
+    def multiply(chunks, s):
+        def one(t, _):
+            lhs, rhs = [], []
+            for k, q in chunks:
+                lhs.append(g[k, q, 0, s].reshape(rows, width))
+                lhs.append(g[k, q, 1, s].reshape(rows, width))
+                index = map_ref[c * points + t, k * points + s]
+                at = pl.ds(pl.multiple_of(q * width, width), width)
+                ur = u[0, index, at, :]
+                ui = u[1, index, at, :]
+                rhs.append(jnp.concatenate([ur, ui], axis=1))
+                rhs.append(jnp.concatenate([-ui, ur], axis=1))
+            acc[t] += jnp.dot(
+                jnp.concatenate(lhs, axis=1),
+                jnp.concatenate(rhs, axis=0),
+                preferred_element_type=jnp.float32,
+            )
+            return 0
+
+        lax.fori_loop(0, points, one, 0)
+
+    def tick(s, _):
+        @pl.when(s < points)
+        def _():
+            for d in range(1, nz):
+                z_copy(d, s, from_energy(d), e).wait_recv()
+            local_copy(s).wait()
+            go = outgoing(s)
+            for kind in (X, Y, P0):
+                go[kind].start()
+
+        @pl.when((s >= 1) & (s < points + 1))
+        def _():
+            r = s - 1
+            come, go = incoming(r), outgoing(r)
+            come[X].wait_recv()
+            go[DA].start()
+            go[PX].start()
+            come[Y].wait_recv()
+            go[DB].start()
+            go[PY].start()
+
+        @pl.when((s >= 2) & (s < points + 2))
+        def _():
+            r = s - 2
+            come, go = incoming(r), outgoing(r)
+            come[DA].wait_recv()
+            come[DB].wait_recv()
+            go[PD].start()
+
+        @pl.when((s >= 1) & (s < points + 1))
+        def _():
+            r = s - 1
+            incoming(r)[P0].wait_recv()
+            multiply(((c, o), (cp, o)), r)
+            multiply(((c, ox), (c, oy)), r)
+
+        @pl.when((s >= 2) & (s < points + 2))
+        def _():
+            r = s - 2
+            come = incoming(r)
+            come[PX].wait_recv()
+            come[PY].wait_recv()
+            multiply(((cp, ox), (cp, oy)), r)
+
+        @pl.when(s >= 3)
+        def _():
+            r = s - 3
+            incoming(r)[PD].wait_recv()
+            multiply(((c, od), (cp, od)), r)
+
+        return 0
+
+    lax.fori_loop(0, points + 3, tick, 0)
+
+    def finish(t, _):
+        for k in range(nz):
+            for part in range(2):
+                values = acc[t, k * tile : (k + 1) * tile, part * width : (part + 1) * width]
+                out[part, k, t, 0] = values.astype(out.dtype)
+        return 0
+
+    lax.fori_loop(0, points, finish, 0)
+
+    def drain(s, _):
+        for d in range(1, nz):
+            z_copy(d, s, e, to_energy(d)).wait_send()
+        go = outgoing(s)
+        for kind in range(8):
+            go[kind].wait_send()
+        return 0
+
+    lax.fori_loop(0, points, drain, 0)
+
+
+def per_device_fused(nz, lesser, coupling, transfer_map):
+    points = lesser.shape[2]
+    tile = lesser.shape[4] // nz
+    width = lesser.shape[5]
+    out_cols = coupling.shape[3]
+    dma = pltpu.SemaphoreType.DMA
+    return pl.pallas_call(
+        functools.partial(kernel, nz),
+        out_shape=jax.ShapeDtypeStruct((2, nz, points, 1, tile, out_cols), jnp.bfloat16),
+        in_specs=[
+            pl.BlockSpec(memory_space=pltpu.SMEM),
+            pl.BlockSpec(memory_space=pl.ANY),
+            pl.BlockSpec(memory_space=pl.ANY),
+        ],
+        out_specs=pl.BlockSpec(memory_space=pltpu.VMEM),
+        scratch_shapes=[
+            pltpu.VMEM((2, 4, 2, points, nz, tile, width), lesser.dtype),
+            pltpu.VMEM(coupling.shape, coupling.dtype),
+            pltpu.VMEM((points, nz * tile, 2 * out_cols), jnp.float32),
+            dma((nz - 1, points)),
+            dma((nz - 1, points)),
+            dma((8, points)),
+            dma((8, points)),
+            dma((points,)),
+            dma(()),
+        ],
+        compiler_params=pltpu.CompilerParams(
+            collective_id=0, has_side_effects=True, vmem_limit_bytes=56 * 1024 * 1024
+        ),
+    )(transfer_map, lesser, coupling)
+
+
 def solution(mesh):
     in_specs = (P(None, "energy", "kpt", None, None, "orb"), P(None, None, None, "orb"), P())
     out_specs = P(None, None, "kpt", None, "energy", "orb")
+    nz = mesh.shape["energy"]
+
+    def per_device(lesser, coupling, transfer_map):
+        shape = lesser.shape
+        fused = (
+            mesh.shape["orb"] == 4
+            and mesh.shape["kpt"] == 2
+            and nz > 1
+            and shape[1] == 1
+            and shape[3] == 1
+            and shape[5] == coupling.shape[3] == 128
+            and shape[4] == nz * 128
+        )
+        if fused:
+            return per_device_fused(nz, lesser, coupling, transfer_map)
+        return per_device_general(lesser, coupling, transfer_map)
+
     return jax.shard_map(
         per_device, mesh=mesh, in_specs=in_specs, out_specs=out_specs, check_vma=False
     )

time: 263 us -> 116 us (0.44)
  Pallas kernels: 0 us -> 111 us
  local copies, waits for them, and re-layouts: 89.2 us -> 3.16 us
  matrix products: 57.7 us -> 0 us
  blocking collectives: 54.3 us -> 0 us
  other arithmetic: 26.3 us -> 0 us
  waiting for transfers between devices: 20.2 us -> 0 us
  between operations: 13.5 us -> 0.01 us
    pallas_call x0 -> x1, Pallas kernels: none -> 111 us  [per_device_fused(): pl.pallas_call(functools.partial(kernel, nz), out_shape=jax.ShapeDtypeStr...]
    gather x2 -> x0, local copies, waits for them, and re-layouts: 59.8 us -> none  [per_device(): selected = jnp.take(coupling, my_columns, axis=1)]
    dot_general x4 -> x0, matrix products: 57.7 us -> none  [the longest x1 15.3 us: complex_terms(): jnp.einsum('prm,tpmj->trj', green[0], selected[0], preferred_element_type...]
    all_to_all x1 -> x0, blocking collectives: 54.3 us -> none  [per_device(): lax.all_to_all(lesser, 'energy', split_axis=4, concat_axis=1, tiled=True)]
    select_n x1 -> x0, other arithmetic: 22.9 us -> none  [per_device(): selected = jnp.take(coupling, my_columns, axis=1)]
    unnamed x3 -> x0, waiting for transfers between devices: 16.6 us -> none
    unnamed x9 -> x1, local copies, waits for them, and re-layouts: 17.2 us -> 3.16 us
    reshape x2 -> x0, local copies, waits for them, and re-layouts: 6.34 us -> none  [per_device(): summed.astype(jnp.bfloat16)]
  transfers between devices with their start and end apart: 2 -> 0, of which waited for: 2 -> 0; matrix products, arithmetic and copies ran while one was open for 32% -> 0% of each run, Pallas kernels for 0% -> 0%
where the time goes in v1:
time: 116 us; the launch traced here: 114 us
  Pallas kernels  111 us (96%)
  local copies, waits for them, and re-layouts  3.16 us (3%)
    pallas_call x1, Pallas kernels, per_device_fused(): pl.pallas_call(functools.partial(kernel, nz), out_shape=jax.ShapeDtypeStr...  111 us
    unnamed x1, local copies, waits for them, and re-layouts  3.16 us

profile of v1, /device:TPU:0, one launch (start us, length us, event | category | flops | bytes accessed | tf_op | source)
XLA Modules:
  0.0 114.3 jit_solution(15360964780550917097)
XLA Ops:
  0.0 111.2 %shard_map.37 = bf16[2,4,8,1,128,128]{5,4,3,2,1,0:T(8,128)(2,1)} custom-call(s32[16,16]{1,0:T(8,128)} %map_ref.1, bf16[2,1,8,1,512,128]{5,4,3,2,1,0:T(8,128)(2,1)} %lesser.1, bf16[2,16,512,128]{3,2,1,0:T(8,128)(2,1)} %coupling.1), custom_call_target="tpu_custom_call" | custom-call | tf_op jit(solution)/shard_map/pallas_call | solution.py:254
  111.2 3.2 %copy.5 = bf16[2,4,8,1,128,128]{5,4,3,2,1,0:T(8,128)(2,1)} copy(bf16[2,4,8,1,128,128]{5,4,3,2,1,0:T(8,128)(2,1)} %shard_map.37) | data formatting | bytes 4194304

commit v2 on v1

--- a/solution.py
+++ b/solution.py
@@ -8,7 +8,8 @@
 from jax.sharding import PartitionSpec as P
 
 MESH = pl.DeviceIdType.MESH
-X, Y, DA, DB, P0, PX, PY, PD = range(8)
+DA, DB, P0, PX, PY, PD = range(6)
+AHEAD = 1
 
 
 def complex_terms(green, selected):
@@ -44,7 +45,7 @@
     return jnp.moveaxis(result, 1, 2)
 
 
-def kernel(nz, map_ref, lesser, coupling, out, g, u, acc, zsend, zrecv, send, recv, local_sem, u_sem):
+def kernel(nz, map_ref, lesser, coupling, out, g, u, acc, zsend, zrecv, osend, orecv, send, recv, local_sem, u_sem):
     points = lesser.shape[2]
     width = lesser.shape[5]
     tile = g.shape[5]
@@ -89,6 +90,30 @@
             device_id_type=MESH,
         )
 
+    def own_copy(way, d, s):
+        owner = from_energy(d)
+        tile_ref = g.at[c, o, :, s, owner]
+        return pltpu.make_async_remote_copy(
+            src_ref=own_rows(s, e) if d == 0 else tile_ref,
+            dst_ref=tile_ref,
+            send_sem=osend.at[way, d, s],
+            recv_sem=orecv.at[way, d, s],
+            device_id=(to_x, to_y)[way],
+            device_id_type=MESH,
+        )
+
+    def wait_own(way, s):
+        for d in range(nz):
+            tile_ref = g.at[c, (ox, oy)[way], :, s, from_energy(d)]
+            pltpu.make_async_remote_copy(
+                src_ref=tile_ref,
+                dst_ref=tile_ref,
+                send_sem=osend.at[way, d, s],
+                recv_sem=orecv.at[way, d, s],
+                device_id=(to_x, to_y)[way],
+                device_id_type=MESH,
+            ).wait_recv()
+
     def block(k, q, s):
         return g.at[k, q, :, s]
 
@@ -97,29 +122,27 @@
 
     to_x, to_y, to_peer = {"orb": ox}, {"orb": oy}, {"kpt": cp}
 
-    def outgoing(s):
-        return {
-            X: move(X, s, block(c, o, s), to_x),
-            Y: move(Y, s, block(c, o, s), to_y),
-            P0: move(P0, s, block(c, o, s), to_peer),
-            DA: move(DA, s, half(ox, 0, s), to_y),
-            PX: move(PX, s, block(c, ox, s), to_peer),
-            DB: move(DB, s, half(oy, 1, s), to_x),
-            PY: move(PY, s, block(c, oy, s), to_peer),
-            PD: move(PD, s, block(c, od, s), to_peer),
+    def outgoing(kind, s):
+        refs = {
+            P0: lambda: block(c, o, s),
+            DA: lambda: half(ox, 0, s),
+            PX: lambda: block(c, ox, s),
+            DB: lambda: half(oy, 1, s),
+            PY: lambda: block(c, oy, s),
+            PD: lambda: block(c, od, s),
         }
-
-    def incoming(s):
-        return {
-            X: move(X, s, block(c, ox, s), to_x),
-            Y: move(Y, s, block(c, oy, s), to_y),
-            DA: move(DA, s, half(od, 0, s), to_y),
-            DB: move(DB, s, half(od, 1, s), to_x),
-            P0: move(P0, s, block(cp, o, s), to_peer),
-            PX: move(PX, s, block(cp, ox, s), to_peer),
-            PY: move(PY, s, block(cp, oy, s), to_peer),
-            PD: move(PD, s, block(cp, od, s), to_peer),
+        return move(kind, s, refs[kind](), {DA: to_y, DB: to_x}.get(kind, to_peer))
+
+    def incoming(kind, s):
+        refs = {
+            DA: lambda: half(od, 0, s),
+            DB: lambda: half(od, 1, s),
+            P0: lambda: block(cp, o, s),
+            PX: lambda: block(cp, ox, s),
+            PY: lambda: block(cp, oy, s),
+            PD: lambda: block(cp, od, s),
         }
+        return move(kind, s, refs[kind](), {DA: to_y, DB: to_x}.get(kind, to_peer))
 
     def locals_start(s, _):
         local_copy(s).start()
@@ -139,6 +162,8 @@
     def z_start(s, _):
         for d in range(1, nz):
             z_copy(d, s, e, to_energy(d)).start()
+        own_copy(0, 0, s).start()
+        own_copy(1, 0, s).start()
         return 0
 
     lax.fori_loop(0, points, z_start, 0)
@@ -169,61 +194,61 @@
             )
             return 0
 
-        lax.fori_loop(0, points, one, 0)
+        lax.fori_loop(0, points, one, 0, unroll=True)
+
+    def lagged(s, lag):
+        return pl.when((s >= lag) & (s < points + lag))
 
     def tick(s, _):
-        @pl.when(s < points)
+        @lagged(s, 0)
         def _():
             for d in range(1, nz):
                 z_copy(d, s, from_energy(d), e).wait_recv()
+                own_copy(0, d, s).start()
+                own_copy(1, d, s).start()
             local_copy(s).wait()
-            go = outgoing(s)
-            for kind in (X, Y, P0):
-                go[kind].start()
-
-        @pl.when((s >= 1) & (s < points + 1))
-        def _():
-            r = s - 1
-            come, go = incoming(r), outgoing(r)
-            come[X].wait_recv()
-            go[DA].start()
-            go[PX].start()
-            come[Y].wait_recv()
-            go[DB].start()
-            go[PY].start()
-
-        @pl.when((s >= 2) & (s < points + 2))
-        def _():
-            r = s - 2
-            come, go = incoming(r), outgoing(r)
-            come[DA].wait_recv()
-            come[DB].wait_recv()
-            go[PD].start()
-
-        @pl.when((s >= 1) & (s < points + 1))
-        def _():
-            r = s - 1
-            incoming(r)[P0].wait_recv()
+            outgoing(P0, s).start()
+
+        @lagged(s, AHEAD)
+        def _():
+            r = s - AHEAD
+            wait_own(0, r)
+            outgoing(DA, r).start()
+            outgoing(PX, r).start()
+            wait_own(1, r)
+            outgoing(DB, r).start()
+            outgoing(PY, r).start()
+
+        @lagged(s, AHEAD + 1)
+        def _():
+            r = s - AHEAD - 1
+            incoming(DA, r).wait_recv()
+            incoming(DB, r).wait_recv()
+            outgoing(PD, r).start()
+
+        @lagged(s, AHEAD)
+        def _():
+            r = s - AHEAD
+            incoming(P0, r).wait_recv()
             multiply(((c, o), (cp, o)), r)
             multiply(((c, ox), (c, oy)), r)
 
-        @pl.when((s >= 2) & (s < points + 2))
-        def _():
-            r = s - 2
-            come = incoming(r)
-            come[PX].wait_recv()
-            come[PY].wait_recv()
+        @lagged(s, AHEAD + 1)
+        def _():
+            r = s - AHEAD - 1
+            incoming(PX, r).wait_recv()
+            incoming(PY, r).wait_recv()
             multiply(((cp, ox), (cp, oy)), r)
 
-        @pl.when(s >= 3)
-        def _():
-            r = s - 3
-            incoming(r)[PD].wait_recv()
+        @lagged(s, AHEAD + 2)
+        def _():
+            r = s - AHEAD - 2
+            incoming(PD, r).wait_recv()
             multiply(((c, od), (cp, od)), r)
 
         return 0
 
-    lax.fori_loop(0, points + 3, tick, 0)
+    lax.fori_loop(0, points + AHEAD + 2, tick, 0)
 
     def finish(t, _):
         for k in range(nz):
@@ -237,9 +262,11 @@
     def drain(s, _):
         for d in range(1, nz):
             z_copy(d, s, e, to_energy(d)).wait_send()
-        go = outgoing(s)
-        for kind in range(8):
-            go[kind].wait_send()
+        for d in range(nz):
+            own_copy(0, d, s).wait_send()
+            own_copy(1, d, s).wait_send()
+        for kind in range(6):
+            outgoing(kind, s).wait_send()
         return 0
 
     lax.fori_loop(0, points, drain, 0)
@@ -266,8 +293,10 @@
             pltpu.VMEM((points, nz * tile, 2 * out_cols), jnp.float32),
             dma((nz - 1, points)),
             dma((nz - 1, points)),
-            dma((8, points)),
-            dma((8, points)),
+            dma((2, nz, points)),
+            dma((2, nz, points)),
+            dma((6, points)),
+            dma((6, points)),
             dma((points,)),
             dma(()),
         ],

time: 116 us -> 91.4 us (0.79); the launches traced: 114 us -> 91.2 us
  Pallas kernels: 111 us -> 88 us
    pallas_call x1, Pallas kernels: 111 us -> 88 us  [per_device_fused(): pl.pallas_call(functools.partial(kernel, nz), out_shape=jax.ShapeDtypeStr...]
where the time goes in v2:
time: 91.4 us; the launch traced here: 91.2 us
  Pallas kernels  88 us (96%)
  local copies, waits for them, and re-layouts  3.16 us (3%)
    pallas_call x1, Pallas kernels, per_device_fused(): pl.pallas_call(functools.partial(kernel, nz), out_shape=jax.ShapeDtypeStr...  88 us
    unnamed x1, local copies, waits for them, and re-layouts  3.16 us

profile of v2, /device:TPU:0, one launch (start us, length us, event | category | flops | bytes accessed | tf_op | source)
XLA Modules:
  0.0 91.2 jit_solution(10589562806412669962)
XLA Ops:
  0.0 88.0 %shard_map.37 = bf16[2,4,8,1,128,128]{5,4,3,2,1,0:T(8,128)(2,1)} custom-call(s32[16,16]{1,0:T(8,128)} %map_ref.1, bf16[2,1,8,1,512,128]{5,4,3,2,1,0:T(8,128)(2,1)} %lesser.1, bf16[2,16,512,128]{3,2,1,0:T(8,128)(2,1)} %coupling.1), custom_call_target="tpu_custom_call" | custom-call | tf_op jit(solution)/shard_map/pallas_call | solution.py:281
  88.0 3.2 %copy.5 = bf16[2,4,8,1,128,128]{5,4,3,2,1,0:T(8,128)(2,1)} copy(bf16[2,4,8,1,128,128]{5,4,3,2,1,0:T(8,128)(2,1)} %shard_map.37) | data formatting | bytes 4194304
